TPU v7x, 32 devices: a whole 2x2x4 slice. The times are simulated.
32 devices in a mesh: gz: 32 (over z, y, x, core).
Axes of the slice: x: 2, y: 2, z: 4, core: 2. Of those that a mesh axis runs over, the one named last changes fastest.
Arguments:
- coefficient: float32 [64, 512, 512], P('gz'), may hold values from 0.2 to 1.3
- initial_field: float32 [64, 512, 512], P('gz'), may hold values from -6 to 6
- observed: float32 [64, 512, 512], P('gz'), may hold values from -6 to 6
- misfit_weight: float32 [64, 512, 512], P('gz'), may hold values from 0.5 to 6, as said below
Outputs:
- coeff_gradient: float32 [64, 512, 512], P('gz')
- adjoint_field: float32 [64, 512, 512], P('gz')
- misfit: float32 [], replicated
Inputs may be any that keep to these rules, and one draw needn't show every extreme that they name: `misfit_weight`: positive cell weights.
All inputs are finite; a program needn't handle non-finite values.
Results may differ from a plain program's by a relative error of at most 0.00002.
Values sent between devices are 32-bit elements; how exact they have to be, the bound alone decides.
A program may use at most 128 MiB of HBM per device.

v0:
```python
import jax
import jax.numpy as jnp
from jax import lax
from jax.sharding import PartitionSpec as P

ITERS = 4


time_step = 0.125


def extended(shard, sides, width):
    for axis, dim in sides:
        count, length = (lax.axis_size(axis), shard.shape[dim])
        up = [(i, (i + 1) % count) for i in range(count - 1)]
        down = [(j, i) for i, j in up]
        last = lax.slice_in_dim(shard, length - width, length, axis=dim)
        initial = lax.slice_in_dim(shard, 0, width, axis=dim)
        before = lax.ppermute(last, axis, up)
        after = lax.ppermute(initial, axis, down)
        shard = jnp.concatenate([before, shard, after], axis=dim)
    return shard


def shifted(block, axis, distance):
    devices = range(lax.axis_size(axis))
    route = [(i - distance, i) for i in devices if i - distance in devices]
    return lax.ppermute(block, axis, route)


def lateral(field):
    padded = jnp.pad(field, ((0, 0), (1, 1), (1, 1)))
    beside = padded[:, 2:, 1:-1] + padded[:, :-2, 1:-1]
    return beside + padded[:, 1:-1, 2:] + padded[:, 1:-1, :-2]


def forward_slope(state):
    padded = extended(state, (("gz", 0),), 1)
    return lateral(state) + padded[2:] + padded[:-2] - 6.0 * state


def adjoint_slope(moved):
    from_above = shifted(moved[0:1], "gz", -1)
    from_below = shifted(moved[-1:], "gz", 1)
    upper = jnp.concatenate([moved[1:], from_above], axis=0)
    lower = jnp.concatenate([from_below, moved[:-1]], axis=0)
    return lateral(moved) + upper + lower - 6.0 * moved


def on_device(coefficient, initial_field, observed, misfit_weight):
    slopes = []
    state = initial_field
    for step in range(ITERS):
        slope = forward_slope(state)
        slopes.append(slope)
        state = state + time_step * coefficient * slope
    resid = state - observed
    weighted = misfit_weight * resid
    total = lax.psum(jnp.sum(weighted * resid), "gz")
    cells = lax.axis_size("gz") * coefficient.shape[0] * coefficient.shape[1] * coefficient.shape[2]
    misfit = jnp.sqrt(total / cells + 1e-06)
    gradient = jnp.zeros_like(coefficient)
    adjoint = weighted
    for step in reversed(range(ITERS)):
        gradient = gradient + time_step * adjoint * slopes[step]
        adjoint = adjoint + time_step * adjoint_slope(coefficient * adjoint)
    gradient = gradient / misfit
    adjoint = adjoint / misfit
    return (gradient, adjoint, misfit)


def solution(mesh):
    placed = (P("gz", None, None), P("gz", None, None), P("gz", None, None), P("gz", None, None))
    return jax.shard_map(
        on_device,
        mesh=mesh,
        in_specs=placed,
        out_specs=(P("gz", None, None), P("gz", None, None), P()),
        check_vma=False,
    )
```

profile of v0, /device:TPU:0, one launch (start us, length us, event | category | flops | bytes accessed | tf_op | source)
XLA Modules:
  0.0 295.9 jit_solution(18146918480263549200)
XLA Ops:
  0.6 0.0 copy-start.4
  0.6 0.0 copy-start
  0.6 1.9 fusion.74
  2.5 1.3 collective-permute-start
  3.8 3.1 %collective-permute-start.1 = (f32[1,512,512]{2,1,0:T(8,128)S(1)}, f32[1,512,512]{2,1,0:T(8,128)S(1)}, u32[]{:S(2)}, u32[]{:S(2)}) collective-permute-start(f32[1,512,512]{2,1,0:T(8,128)S(1)} %get-tuple-element.36), channel_id=1, source_target_pairs={{0,1},{1,2},{2,3},{3,4},{4,5},{5,6},{6,7},{7,8},{8,9},{9,10},{10,1... | collective-permute-start | bytes 3145736 | tf_op jit(solution)/shard_map/ppermute | solution.py:19
  6.9 0.1 collective-permute-done
  7.1 2.1 collective-permute-done.1
  9.1 0.0 copy-done.4
  9.1 0.0 copy-done
  9.1 3.2 %multiply_add_fusion.2 = (f32[2,512,512]{2,1,0:T(8,128)S(1)}, f32[2,512,512]{2,1,0:T(8,128)}) fusion(f32[2,512,512]{2,1,0:T(8,128)S(1)} %copy-done.4, f32[2,512,512]{2,1,0:T(8,128)S(1)} %copy-done, f32[1,512,512]{2,1,0:T(8,128)S(1)} %collective-permute-done.1, f32[1,512,512]{2,1,0:T(8,128)S(1)} %collective-permute-done), kind=kLoop, calls=%fused_computation.102 | loop fusion | flops 6291456 | bytes 10485760 | tf_op jit(solution)/shard_map/add | solution.py:56
  12.3 0.2 fusion.73
  12.5 1.3 collective-permute-start.2
  13.8 25.8 %collective-permute-start.3 = (f32[1,512,512]{2,1,0:T(8,128)S(1)}, f32[1,512,512]{2,1,0:T(8,128)S(1)}, u32[]{:S(2)}, u32[]{:S(2)}) collective-permute-start(f32[1,512,512]{2,1,0:T(8,128)S(1)} %get-tuple-element.34), channel_id=1, source_target_pairs={{0,1},{1,2},{2,3},{3,4},{4,5},{5,6},{6,7},{7,8},{8,9},{9,10},{10,1... | collective-permute-start | bytes 3145736 | tf_op jit(solution)/shard_map/ppermute | solution.py:19
  39.6 0.1 collective-permute-done.2
  39.8 2.1 collective-permute-done.3
  41.8 3.2 %multiply_add_fusion.1 = (f32[2,512,512]{2,1,0:T(8,128)S(1)}, f32[2,512,512]{2,1,0:T(8,128)}) fusion(f32[2,512,512]{2,1,0:T(8,128)S(1)} %get-tuple-element.17, f32[2,512,512]{2,1,0:T(8,128)S(1)} %copy-done, f32[1,512,512]{2,1,0:T(8,128)S(1)} %collective-permute-done.3, f32[1,512,512]{2,1,0:T(8,128)S(1)} %collective-permute-done.2), kind=kLoop, calls=%fused_computation.101 | loop fusion | flops 6291456 | bytes 10485760 | tf_op jit(solution)/shard_map/add | solution.py:56
  45.0 0.2 fusion.72
  45.2 1.3 collective-permute-start.4
  46.5 22.9 %collective-permute-start.5 = (f32[1,512,512]{2,1,0:T(8,128)S(1)}, f32[1,512,512]{2,1,0:T(8,128)S(1)}, u32[]{:S(2)}, u32[]{:S(2)}) collective-permute-start(f32[1,512,512]{2,1,0:T(8,128)S(1)} %get-tuple-element.32), channel_id=1, source_target_pairs={{0,1},{1,2},{2,3},{3,4},{4,5},{5,6},{6,7},{7,8},{8,9},{9,10},{10,1... | collective-permute-start | bytes 3145736 | tf_op jit(solution)/shard_map/ppermute | solution.py:19
  69.3 0.1 collective-permute-done.4
  69.5 2.1 collective-permute-done.5
  71.6 3.2 %multiply_add_fusion = (f32[2,512,512]{2,1,0:T(8,128)S(1)}, f32[2,512,512]{2,1,0:T(8,128)}) fusion(f32[2,512,512]{2,1,0:T(8,128)S(1)} %get-tuple-element.15, f32[2,512,512]{2,1,0:T(8,128)S(1)} %copy-done, f32[1,512,512]{2,1,0:T(8,128)S(1)} %collective-permute-done.5, f32[1,512,512]{2,1,0:T(8,128)S(1)} %collective-permute-done.4), kind=kLoop, calls=%fused_computation.100 | loop fusion | flops 6291456 | bytes 10485760 | tf_op jit(solution)/shard_map/add | solution.py:56
  74.8 0.0 copy-start.6
  74.8 0.2 fusion.71
  74.9 1.4 collective-permute-start.6
  76.4 0.0 copy-start.5
  76.4 19.4 %collective-permute-start.7 = (f32[1,512,512]{2,1,0:T(8,128)S(1)}, f32[1,512,512]{2,1,0:T(8,128)S(1)}, u32[]{:S(2)}, u32[]{:S(2)}) collective-permute-start(f32[1,512,512]{2,1,0:T(8,128)S(1)} %get-tuple-element.30), channel_id=1, source_target_pairs={{0,1},{1,2},{2,3},{3,4},{4,5},{5,6},{6,7},{7,8},{8,9},{9,10},{10,1... | collective-permute-start | bytes 3145736 | tf_op jit(solution)/shard_map/ppermute | solution.py:19
  95.8 0.0 collective-permute-done.6
  95.8 2.2 collective-permute-done.7
  98.0 0.0 copy-done.6
  98.0 3.6 %add_subtract_fusion = (f32[2,512,512]{2,1,0:T(8,128)S(1)}, f32[2,512,512]{2,1,0:T(8,128)}) fusion(f32[2,512,512]{2,1,0:T(8,128)S(1)} %copy-done.6, f32[2,512,512]{2,1,0:T(8,128)S(1)} %get-tuple-element.13, f32[2,512,512]{2,1,0:T(8,128)S(1)} %copy-done, f32[1,512,512]{2,1,0:T(8,128)S(1)} %collective-permute-done.7, f32[1,512,512]{2,1,0:T(8,128)S(1)} %collective-permute-done.6), kind=kLoop, calls=%fused_computation.99 | loop fusion | flops 6815744 | bytes 12582912 | tf_op jit(solution)/shard_map/sub | solution.py:57
  101.6 0.0 copy-done.5
  101.6 1.2 multiply_reduce_fusion
  102.8 0.5 mul.108
  103.3 0.2 fusion.70
  103.4 17.4 %collective-permute-start.9 = (f32[1,512,512]{2,1,0:T(8,128)S(1)}, f32[1,512,512]{2,1,0:T(8,128)S(1)}, u32[]{:S(2)}, u32[]{:S(2)}) collective-permute-start(f32[1,512,512]{2,1,0:T(8,128)S(1)} %get-tuple-element.27), channel_id=1, source_target_pairs={{0,1},{1,2},{2,3},{3,4},{4,5},{5,6},{6,7},{7,8},{8,9},{9,10},{10,1... | collective-permute-start | bytes 3145736 | tf_op jit(solution)/shard_map/ppermute | solution.py:28
  120.9 1.3 collective-permute-start.8
  122.2 0.9 collective-permute-done.9
  123.1 4.3 %collective-permute-done.8 = f32[1,512,512]{2,1,0:T(8,128)S(1)} collective-permute-done((f32[1,512,512]{2,1,0:T(8,128)S(1)}, f32[1,512,512]{2,1,0:T(8,128)S(1)}, u32[]{:S(2)}, u32[]{:S(2)}) %collective-permute-start.8) | collective-permute-done | bytes 1048608 | tf_op jit(solution)/shard_map/ppermute | solution.py:28
  127.4 2.4 fusion.61
  129.7 0.0 copy-start.1
  129.8 0.2 fusion.69
  129.9 28.2 %collective-permute-start.11 = (f32[1,512,512]{2,1,0:T(8,128)S(1)}, f32[1,512,512]{2,1,0:T(8,128)S(1)}, u32[]{:S(2)}, u32[]{:S(2)}) collective-permute-start(f32[1,512,512]{2,1,0:T(8,128)S(1)} %get-tuple-element.25), channel_id=1, source_target_pairs={{0,1},{1,2},{2,3},{3,4},{4,5},{5,6},{6,7},{7,8},{8,9},{9,10},{10,1... | collective-permute-start | bytes 3145736 | tf_op jit(solution)/shard_map/ppermute | solution.py:28
  158.2 1.3 collective-permute-start.10
  159.5 0.9 collective-permute-done.11
  160.4 2.4 collective-permute-done.10
  162.7 2.4 fusion.59
  165.1 0.0 copy-done.1
  165.1 0.0 copy-start.2
  165.1 0.2 fusion.68
  165.3 25.7 %collective-permute-start.13 = (f32[1,512,512]{2,1,0:T(8,128)S(1)}, f32[1,512,512]{2,1,0:T(8,128)S(1)}, u32[]{:S(2)}, u32[]{:S(2)}) collective-permute-start(f32[1,512,512]{2,1,0:T(8,128)S(1)} %get-tuple-element.23), channel_id=1, source_target_pairs={{0,1},{1,2},{2,3},{3,4},{4,5},{5,6},{6,7},{7,8},{8,9},{9,10},{10,1... | collective-permute-start | bytes 3145736 | tf_op jit(solution)/shard_map/ppermute | solution.py:28
  191.0 1.5 collective-permute-start.12
  192.5 0.7 collective-permute-done.13
  193.2 2.4 collective-permute-done.12
  195.6 3.4 %fusion.57 = (f32[2,512,512]{2,1,0:T(8,128)S(1)}, f32[2,512,512]{2,1,0:T(8,128)}) fusion(f32[2,512,512]{2,1,0:T(8,128)S(1)} %copy-done, f32[2,512,512]{2,1,0:T(8,128)S(1)} %get-tuple-element.8, f32[2,512,512]{2,1,0:T(8,128)S(1)} %get-tuple-element.7, f32[1,512,512]{2,1,0:T(8,128)S(1)} %get-tuple-element.24, f32[1,512,512]{2,1,0:T(8,128)S(1)} %collective-permute-done.13, ...), kind=kLoop, calls=%fused_computation.103 | loop fusion | flops 6291456 | bytes 14680064 | tf_op jit(solution)/shard_map/mul | solution.py:66
  199.0 0.0 copy-done.2
  199.0 1.4 copy-done.3
  200.4 1.2 fusion.67
  201.6 23.6 %collective-permute-start.15 = (f32[1,512,512]{2,1,0:T(8,128)S(1)}, f32[1,512,512]{2,1,0:T(8,128)}, u32[]{:S(2)}, u32[]{:S(2)}) collective-permute-start(f32[1,512,512]{2,1,0:T(8,128)S(1)} %get-tuple-element.21), channel_id=1, source_target_pairs={{0,1},{1,2},{2,3},{3,4},{4,5},{5,6},{6,7},{7,8},{8,9},{9,10},{10,1... | collective-permute-start | bytes 3145736 | tf_op jit(solution)/shard_map/ppermute | solution.py:28
  225.1 1.3 collective-permute-start.14
  226.4 54.6 %psum.7 = f32[]{:T(128)} all-reduce(f32[]{:T(128)} %get-tuple-element.5), channel_id=1, replica_groups=mesh['gz'=32] {'gz'}, use_global_device_ids=true, to_apply=%region_1.2 | all-reduce | flops 1 | bytes 8 | tf_op jit(solution)/shard_map/psum | solution.py:59
  281.7 0.0 collective-permute-done.15
  281.7 0.0 collective-permute-done.14
  281.7 13.1 %fusion.56 = (f32[2,512,512]{2,1,0:T(8,128)}, f32[2,512,512]{2,1,0:T(8,128)}) fusion(f32[2,512,512]{2,1,0:T(8,128)} %get-tuple-element.4, f32[2,512,512]{2,1,0:T(8,128)} %copy-done.3, f32[1,512,512]{2,1,0:T(8,128)} %collective-permute-done.14, f32[1,512,512]{2,1,0:T(8,128)S(1)} %get-tuple-element.21, f32[1,512,512]{2,1,0:T(8,128)} %get-tuple-element.22, ...), kind=kLoop, calls=%fused_computation.88 | loop fusion | flops 12582912 | bytes 27262980 | tf_op jit(solution)/shard_map/div | solution.py:68
  (1 shorter events, 0.0 us)
Async XLA Ops:
  0.6 8.5 %copy-start.4 = (f32[2,512,512]{2,1,0:T(8,128)S(1)}, f32[2,512,512]{2,1,0:T(8,128)}, u32[]{:S(2)}) copy-start(f32[2,512,512]{2,1,0:T(8,128)} %param.5) | copy-start | bytes 6291460
  0.6 8.5 %copy-start = (f32[2,512,512]{2,1,0:T(8,128)S(1)}, f32[2,512,512]{2,1,0:T(8,128)}, u32[]{:S(2)}) copy-start(f32[2,512,512]{2,1,0:T(8,128)} %param.4) | copy-start | bytes 6291460
  2.5 4.6 %collective-permute-start = (f32[1,512,512]{2,1,0:T(8,128)S(1)}, f32[1,512,512]{2,1,0:T(8,128)S(1)}, u32[]{:S(2)}, u32[]{:S(2)}) collective-permute-start(f32[1,512,512]{2,1,0:T(8,128)S(1)} %get-tuple-element.35), channel_id=1, source_target_pairs={{1,0},{2,1},{3,2},{4,3},{5,4},{6,5},{7,6},{8,7},{9,8},{10,9},{11,1... | collective-permute-start | bytes 3145736 | tf_op jit(solution)/shard_map/ppermute | solution.py:20
  3.8 5.3 %collective-permute-start.1 = (f32[1,512,512]{2,1,0:T(8,128)S(1)}, f32[1,512,512]{2,1,0:T(8,128)S(1)}, u32[]{:S(2)}, u32[]{:S(2)}) collective-permute-start(f32[1,512,512]{2,1,0:T(8,128)S(1)} %get-tuple-element.36), channel_id=1, source_target_pairs={{0,1},{1,2},{2,3},{3,4},{4,5},{5,6},{6,7},{7,8},{8,9},{9,10},{10,1... | collective-permute-start | bytes 3145736 | tf_op jit(solution)/shard_map/ppermute | solution.py:19
  12.5 27.3 %collective-permute-start.2 = (f32[1,512,512]{2,1,0:T(8,128)S(1)}, f32[1,512,512]{2,1,0:T(8,128)S(1)}, u32[]{:S(2)}, u32[]{:S(2)}) collective-permute-start(f32[1,512,512]{2,1,0:T(8,128)S(1)} %get-tuple-element.33), channel_id=1, source_target_pairs={{1,0},{2,1},{3,2},{4,3},{5,4},{6,5},{7,6},{8,7},{9,8},{10,9},{11,1... | collective-permute-start | bytes 3145736 | tf_op jit(solution)/shard_map/ppermute | solution.py:20
  13.8 28.0 %collective-permute-start.3 = (f32[1,512,512]{2,1,0:T(8,128)S(1)}, f32[1,512,512]{2,1,0:T(8,128)S(1)}, u32[]{:S(2)}, u32[]{:S(2)}) collective-permute-start(f32[1,512,512]{2,1,0:T(8,128)S(1)} %get-tuple-element.34), channel_id=1, source_target_pairs={{0,1},{1,2},{2,3},{3,4},{4,5},{5,6},{6,7},{7,8},{8,9},{9,10},{10,1... | collective-permute-start | bytes 3145736 | tf_op jit(solution)/shard_map/ppermute | solution.py:19
  45.2 24.3 %collective-permute-start.4 = (f32[1,512,512]{2,1,0:T(8,128)S(1)}, f32[1,512,512]{2,1,0:T(8,128)S(1)}, u32[]{:S(2)}, u32[]{:S(2)}) collective-permute-start(f32[1,512,512]{2,1,0:T(8,128)S(1)} %get-tuple-element.31), channel_id=1, source_target_pairs={{1,0},{2,1},{3,2},{4,3},{5,4},{6,5},{7,6},{8,7},{9,8},{10,9},{11,1... | collective-permute-start | bytes 3145736 | tf_op jit(solution)/shard_map/ppermute | solution.py:20
  46.5 25.1 %collective-permute-start.5 = (f32[1,512,512]{2,1,0:T(8,128)S(1)}, f32[1,512,512]{2,1,0:T(8,128)S(1)}, u32[]{:S(2)}, u32[]{:S(2)}) collective-permute-start(f32[1,512,512]{2,1,0:T(8,128)S(1)} %get-tuple-element.32), channel_id=1, source_target_pairs={{0,1},{1,2},{2,3},{3,4},{4,5},{5,6},{6,7},{7,8},{8,9},{9,10},{10,1... | collective-permute-start | bytes 3145736 | tf_op jit(solution)/shard_map/ppermute | solution.py:19
  74.8 23.2 %copy-start.6 = (f32[2,512,512]{2,1,0:T(8,128)S(1)}, f32[2,512,512]{2,1,0:T(8,128)}, u32[]{:S(2)}) copy-start(f32[2,512,512]{2,1,0:T(8,128)} %param.6) | copy-start | bytes 6291460
  74.9 20.9 %collective-permute-start.6 = (f32[1,512,512]{2,1,0:T(8,128)S(1)}, f32[1,512,512]{2,1,0:T(8,128)S(1)}, u32[]{:S(2)}, u32[]{:S(2)}) collective-permute-start(f32[1,512,512]{2,1,0:T(8,128)S(1)} %get-tuple-element.29), channel_id=1, source_target_pairs={{1,0},{2,1},{3,2},{4,3},{5,4},{6,5},{7,6},{8,7},{9,8},{10,9},{11,1... | collective-permute-start | bytes 3145736 | tf_op jit(solution)/shard_map/ppermute | solution.py:20
  76.4 25.2 %copy-start.5 = (f32[2,512,512]{2,1,0:T(8,128)S(1)}, f32[2,512,512]{2,1,0:T(8,128)}, u32[]{:S(2)}) copy-start(f32[2,512,512]{2,1,0:T(8,128)} %param.7) | copy-start | bytes 6291460
  76.4 21.6 %collective-permute-start.7 = (f32[1,512,512]{2,1,0:T(8,128)S(1)}, f32[1,512,512]{2,1,0:T(8,128)S(1)}, u32[]{:S(2)}, u32[]{:S(2)}) collective-permute-start(f32[1,512,512]{2,1,0:T(8,128)S(1)} %get-tuple-element.30), channel_id=1, source_target_pairs={{0,1},{1,2},{2,3},{3,4},{4,5},{5,6},{6,7},{7,8},{8,9},{9,10},{10,1... | collective-permute-start | bytes 3145736 | tf_op jit(solution)/shard_map/ppermute | solution.py:19
  103.4 19.7 %collective-permute-start.9 = (f32[1,512,512]{2,1,0:T(8,128)S(1)}, f32[1,512,512]{2,1,0:T(8,128)S(1)}, u32[]{:S(2)}, u32[]{:S(2)}) collective-permute-start(f32[1,512,512]{2,1,0:T(8,128)S(1)} %get-tuple-element.27), channel_id=1, source_target_pairs={{0,1},{1,2},{2,3},{3,4},{4,5},{5,6},{6,7},{7,8},{8,9},{9,10},{10,1... | collective-permute-start | bytes 3145736 | tf_op jit(solution)/shard_map/ppermute | solution.py:28
  120.9 6.5 %collective-permute-start.8 = (f32[1,512,512]{2,1,0:T(8,128)S(1)}, f32[1,512,512]{2,1,0:T(8,128)S(1)}, u32[]{:S(2)}, u32[]{:S(2)}) collective-permute-start(f32[1,512,512]{2,1,0:T(8,128)S(1)} %get-tuple-element.28), channel_id=1, source_target_pairs={{1,0},{2,1},{3,2},{4,3},{5,4},{6,5},{7,6},{8,7},{9,8},{10,9},{11,1... | collective-permute-start | bytes 3145736 | tf_op jit(solution)/shard_map/ppermute | solution.py:28
  129.7 35.4 %copy-start.1 = (f32[2,512,512]{2,1,0:T(8,128)}, f32[2,512,512]{2,1,0:T(8,128)S(1)}, u32[]{:S(2)}) copy-start(f32[2,512,512]{2,1,0:T(8,128)S(1)} %get-tuple-element.10) | copy-start | bytes 6291460
  129.9 30.4 %collective-permute-start.11 = (f32[1,512,512]{2,1,0:T(8,128)S(1)}, f32[1,512,512]{2,1,0:T(8,128)S(1)}, u32[]{:S(2)}, u32[]{:S(2)}) collective-permute-start(f32[1,512,512]{2,1,0:T(8,128)S(1)} %get-tuple-element.25), channel_id=1, source_target_pairs={{0,1},{1,2},{2,3},{3,4},{4,5},{5,6},{6,7},{7,8},{8,9},{9,10},{10,1... | collective-permute-start | bytes 3145736 | tf_op jit(solution)/shard_map/ppermute | solution.py:28
  158.2 4.6 %collective-permute-start.10 = (f32[1,512,512]{2,1,0:T(8,128)S(1)}, f32[1,512,512]{2,1,0:T(8,128)S(1)}, u32[]{:S(2)}, u32[]{:S(2)}) collective-permute-start(f32[1,512,512]{2,1,0:T(8,128)S(1)} %get-tuple-element.26), channel_id=1, source_target_pairs={{1,0},{2,1},{3,2},{4,3},{5,4},{6,5},{7,6},{8,7},{9,8},{10,9},{11,1... | collective-permute-start | bytes 3145736 | tf_op jit(solution)/shard_map/ppermute | solution.py:28
  165.1 33.9 %copy-start.2 = (f32[2,512,512]{2,1,0:T(8,128)}, f32[2,512,512]{2,1,0:T(8,128)S(1)}, u32[]{:S(2)}) copy-start(f32[2,512,512]{2,1,0:T(8,128)S(1)} %get-tuple-element.8) | copy-start | bytes 6291460
  165.3 27.9 %collective-permute-start.13 = (f32[1,512,512]{2,1,0:T(8,128)S(1)}, f32[1,512,512]{2,1,0:T(8,128)S(1)}, u32[]{:S(2)}, u32[]{:S(2)}) collective-permute-start(f32[1,512,512]{2,1,0:T(8,128)S(1)} %get-tuple-element.23), channel_id=1, source_target_pairs={{0,1},{1,2},{2,3},{3,4},{4,5},{5,6},{6,7},{7,8},{8,9},{9,10},{10,1... | collective-permute-start | bytes 3145736 | tf_op jit(solution)/shard_map/ppermute | solution.py:28
  191.0 4.6 %collective-permute-start.12 = (f32[1,512,512]{2,1,0:T(8,128)S(1)}, f32[1,512,512]{2,1,0:T(8,128)S(1)}, u32[]{:S(2)}, u32[]{:S(2)}) collective-permute-start(f32[1,512,512]{2,1,0:T(8,128)S(1)} %get-tuple-element.24), channel_id=1, source_target_pairs={{1,0},{2,1},{3,2},{4,3},{5,4},{6,5},{7,6},{8,7},{9,8},{10,9},{11,1... | collective-permute-start | bytes 3145736 | tf_op jit(solution)/shard_map/ppermute | solution.py:28
  199.0 1.4 copy-start.3
  201.6 80.1 %collective-permute-start.15 = (f32[1,512,512]{2,1,0:T(8,128)S(1)}, f32[1,512,512]{2,1,0:T(8,128)}, u32[]{:S(2)}, u32[]{:S(2)}) collective-permute-start(f32[1,512,512]{2,1,0:T(8,128)S(1)} %get-tuple-element.21), channel_id=1, source_target_pairs={{0,1},{1,2},{2,3},{3,4},{4,5},{5,6},{6,7},{7,8},{8,9},{9,10},{10,1... | collective-permute-start | bytes 3145736 | tf_op jit(solution)/shard_map/ppermute | solution.py:28
  225.1 56.6 %collective-permute-start.14 = (f32[1,512,512]{2,1,0:T(8,128)}, f32[1,512,512]{2,1,0:T(8,128)}, u32[]{:S(2)}, u32[]{:S(2)}) collective-permute-start(f32[1,512,512]{2,1,0:T(8,128)} %get-tuple-element.22), channel_id=1, source_target_pairs={{1,0},{2,1},{3,2},{4,3},{5,4},{6,5},{7,6},{8,7},{9,8},{10,9},{11,1... | collective-permute-start | bytes 3145736 | tf_op jit(solution)/shard_map/ppermute | solution.py:28
where the time goes:
time: 297 us; the launch traced here: 296 us
  starting transfers between devices  177 us (60%)
  blocking collectives  54.6 us (18%)
  other arithmetic  36.1 us (12%)
  waiting for transfers between devices  20.3 us (7%)
  local copies, waits for them, and re-layouts  5.49 us (2%)
    ppermute x8, starting transfers between devices, shifted(): return lax.ppermute(block, axis, route)  100 us
    ppermute x4, starting transfers between devices, extended(): before = lax.ppermute(last, axis, up)  71.2 us
    psum x1, blocking collectives, on_device(): total = lax.psum(jnp.sum(weighted * resid), 'gz')  54.6 us
    div x1, other arithmetic, on_device(): adjoint = adjoint / misfit  13.1 us
    ppermute x8, waiting for transfers between devices, shifted(): return lax.ppermute(block, axis, route)  11.5 us
    add x3, other arithmetic, on_device(): state = state + time_step * coefficient * slope  9.57 us
    mul x4, other arithmetic, on_device(): adjoint = adjoint + time_step * adjoint_slope(coefficient * adjoint)  8.65 us
    ppermute x4, waiting for transfers between devices, extended(): before = lax.ppermute(last, axis, up)  8.35 us
  transfers between devices with their start and end apart: 16, of which 13 were waited for; matrix products, arithmetic and copies ran while one was open for 0% of the time, Pallas kernels for 0%

commit v1 on v0

v1 whole, which is shorter than its diff:
```python
import functools

import jax
import jax.numpy as jnp
from jax import lax
from jax.experimental import pallas as pl
from jax.experimental.pallas import tpu as pltpu
from jax.sharding import PartitionSpec as P

ITERS = 4
time_step = 0.125
MESH = pl.DeviceIdType.MESH
PAD = 8
CHUNKS = 8
TILE = 16


def kernel(n, rounds, cells, coef_hbm, init_hbm, obs_hbm, wgt_hbm, grad, adj, misfit_out,
           st, sl, halo, coef, obs, wgt, part, send_sem, recv_sem, psend_sem, precv_sem, load_sem):
    planes, ny, nx = coef_hbm.shape
    rows = ny // CHUNKS
    exchanges = 2 * ITERS
    me = lax.axis_index("gz")
    has_lo = me > 0
    has_hi = me < n - 1

    loads = [
        pltpu.make_async_copy(init_hbm, st.at[0, :, pl.ds(PAD, ny), :], load_sem.at[0]),
        pltpu.make_async_copy(coef_hbm, coef, load_sem.at[1]),
        pltpu.make_async_copy(obs_hbm, obs, load_sem.at[2]),
        pltpu.make_async_copy(wgt_hbm, wgt, load_sem.at[3]),
    ]

    partners = []
    for r in range(rounds):
        bit = 1 << r
        partners.append(me + bit * (1 - 2 * ((me // bit) % 2)))

    barrier = pltpu.get_barrier_semaphore()

    def greet(device):
        pl.semaphore_signal(barrier, inc=1, device_id=(device,), device_id_type=MESH)

    @pl.when(has_lo)
    def _():
        greet(me - 1)

    @pl.when(has_hi)
    def _():
        greet(me + 1)

    for partner in partners[1:]:
        greet(partner)
    for load in loads:
        load.start()

    zero_rows = jnp.zeros((PAD, nx), jnp.float32)

    def clear_pad(e, carry):
        for p in range(planes):
            st[e, p, pl.ds(0, PAD), :] = zero_rows
            st[e, p, pl.ds(PAD + ny, PAD), :] = zero_rows
        return carry

    lax.fori_loop(0, exchanges, clear_pad, 0)

    def clear_halo(side):
        def clear(i, carry):
            e = i // (ny // PAD)
            row = pl.multiple_of((i % (ny // PAD)) * PAD, PAD)
            halo[side, e, pl.ds(row, PAD), :] = zero_rows
            return carry

        lax.fori_loop(0, exchanges * (ny // PAD), clear, 0)

    @pl.when(me == 0)
    def _():
        clear_halo(0)

    @pl.when(me == n - 1)
    def _():
        clear_halo(1)

    @pl.when(has_lo & has_hi)
    def _():
        pl.semaphore_wait(barrier, rounds + 1)

    if rounds:
        @pl.when((me == 0) | (me == n - 1))
        def _():
            pl.semaphore_wait(barrier, rounds)

    def remote(side, e, j, src):
        at = pl.ds(pl.multiple_of(j * rows, rows), rows)
        return pltpu.make_async_remote_copy(
            src_ref=src,
            dst_ref=halo.at[side, e, at, :],
            send_sem=send_sem.at[side, e, j],
            recv_sem=recv_sem.at[side, e, j],
            device_id=(me + 1 - 2 * side,),
            device_id_type=MESH,
        )

    def source(side, e, j):
        at = pl.ds(pl.multiple_of(PAD + j * rows, PAD), rows)
        return st.at[e, (planes - 1) * (1 - side), at, :]

    def first_source(side, j):
        return init_hbm.at[(planes - 1) * (1 - side), pl.ds(pl.multiple_of(j * rows, rows), rows), :]

    def send_first(j, carry):
        @pl.when(has_hi)
        def _():
            remote(0, 0, j, first_source(0, j)).start()

        @pl.when(has_lo)
        def _():
            remote(1, 0, j, first_source(1, j)).start()

        return carry

    lax.fori_loop(0, CHUNKS, send_first, 0)

    def send(e, j):
        @pl.when(has_hi)
        def _():
            remote(0, e, j, source(0, e, j)).start()

        @pl.when(has_lo)
        def _():
            remote(1, e, j, source(1, e, j)).start()

    def receive(e, j):
        @pl.when(has_lo)
        def _():
            remote(0, e, j, source(0, e, j)).wait_recv()

        @pl.when(has_hi)
        def _():
            remote(1, e, j, source(1, e, j)).wait_recv()

    lane = lax.broadcasted_iota(jnp.int32, (TILE, nx), 1)
    leftmost = lane == 0
    rightmost = lane == nx - 1

    def tile_laplace(e, row):
        here = pl.ds(row, TILE)
        tall = [st[e, p, pl.ds(row, TILE + 2 * PAD), :] for p in range(planes)]
        mids = [t[PAD:PAD + TILE] for t in tall]
        result = []
        for p in range(planes):
            mid = mids[p]
            beside = tall[p][PAD + 1:PAD + 1 + TILE] + tall[p][PAD - 1:PAD - 1 + TILE]
            beside = beside + jnp.where(rightmost, 0.0, pltpu.roll(mid, nx - 1, 1))
            beside = beside + jnp.where(leftmost, 0.0, pltpu.roll(mid, 1, 1))
            above = mids[p + 1] if p + 1 < planes else halo[1, e, here, :]
            below = mids[p - 1] if p > 0 else halo[0, e, here, :]
            result.append((mid, beside + above + below - 6.0 * mid))
        return result

    def over_tiles(j, body, carry):
        def one(t, carry):
            row = pl.multiple_of(j * rows + t * TILE, TILE)
            return body(row, carry)

        return lax.fori_loop(0, rows // TILE, one, carry)

    loads[0].wait()
    loads[1].wait()

    def forward(e, carry):
        def chunk(j, carry):
            receive(e, j)

            def body(row, carry):
                here, padded = pl.ds(row, TILE), pl.ds(pl.multiple_of(row + PAD, PAD), TILE)
                for p, (mid, slope) in enumerate(tile_laplace(e, row)):
                    sl[e, p, here, :] = slope
                    st[e + 1, p, padded, :] = mid + time_step * coef[p, here, :] * slope
                return carry

            over_tiles(j, body, 0)
            send(e + 1, j)
            return carry

        return lax.fori_loop(0, CHUNKS, chunk, carry)

    lax.fori_loop(0, ITERS - 1, forward, 0)
    loads[2].wait()
    loads[3].wait()

    last = ITERS - 1

    def turn(j, total):
        receive(last, j)

        def body(row, total):
            here, padded = pl.ds(row, TILE), pl.ds(pl.multiple_of(row + PAD, PAD), TILE)
            for p, (mid, slope) in enumerate(tile_laplace(last, row)):
                c = coef[p, here, :]
                resid = mid + time_step * c * slope - obs[p, here, :]
                weighted = wgt[p, here, :] * resid
                total = total + weighted * resid
                adj[p, here, :] = weighted
                grad[p, here, :] = time_step * weighted * slope
                st[ITERS, p, padded, :] = c * weighted
            return total

        total = over_tiles(j, body, total)
        send(ITERS, j)
        return total

    total = lax.fori_loop(0, CHUNKS, turn, jnp.zeros((TILE, nx), jnp.float32))
    folded = total[0:8]
    for i in range(1, TILE // 8):
        folded = folded + total[8 * i:8 * i + 8]
    narrow = folded[:, 0:128]
    for i in range(1, nx // 128):
        narrow = narrow + folded[:, 128 * i:128 * i + 128]
    part[0] = narrow

    def exchange(r):
        return pltpu.make_async_remote_copy(
            src_ref=part.at[2 * r],
            dst_ref=part.at[2 * r + 1],
            send_sem=psend_sem.at[r],
            recv_sem=precv_sem.at[r],
            device_id=(partners[r],),
            device_id_type=MESH,
        )

    def adjoint_chunk(e, j):
        receive(e, j)

        def body(row, carry):
            here, padded = pl.ds(row, TILE), pl.ds(pl.multiple_of(row + PAD, PAD), TILE)
            for p, (_, change) in enumerate(tile_laplace(e, row)):
                lam = adj[p, here, :] + time_step * change
                adj[p, here, :] = lam
                grad[p, here, :] = grad[p, here, :] + time_step * lam * sl[exchanges - 2 - e, p, here, :]
                st[e + 1, p, padded, :] = coef[p, here, :] * lam
            return carry

        over_tiles(j, body, 0)
        send(e + 1, j)

    done = 0
    for j in range(CHUNKS):
        adjoint_chunk(ITERS, j)
        if j < rounds:
            if j > 0:
                exchange(j - 1).wait_recv()
                part[2 * j] = part[2 * j - 2] + part[2 * j - 1]
            exchange(j).start()
            done = j + 1
    for r in range(done, rounds):
        exchange(r - 1).wait_recv()
        part[2 * r] = part[2 * r - 2] + part[2 * r - 1]
        exchange(r).start()

    def backward(e, carry):
        def chunk(j, carry):
            adjoint_chunk(e, j)
            return carry

        return lax.fori_loop(0, CHUNKS, chunk, carry)

    lax.fori_loop(ITERS + 1, exchanges - 1, backward, 0)

    if rounds:
        exchange(rounds - 1).wait_recv()
        whole = part[2 * rounds - 2] + part[2 * rounds - 1]
    else:
        whole = part[0]
    whole = jnp.sum(jnp.sum(whole, axis=1, keepdims=True), axis=0, keepdims=True)
    misfit = jnp.sqrt(jnp.broadcast_to(whole, (8, 128)) / cells + 1e-06)
    misfit_out[...] = misfit

    def final(j, carry):
        receive(exchanges - 1, j)

        def body(row, carry):
            here = pl.ds(row, TILE)
            for p, (_, change) in enumerate(tile_laplace(exchanges - 1, row)):
                adj[p, here, :] = adj[p, here, :] + time_step * change
            return carry

        return over_tiles(j, body, carry)

    lax.fori_loop(0, CHUNKS, final, 0)

    def drain(j, carry):
        for e in range(exchanges):
            @pl.when(has_hi)
            def _():
                remote(0, e, j, first_source(0, j) if e == 0 else source(0, e, j)).wait_send()

            @pl.when(has_lo)
            def _():
                remote(1, e, j, first_source(1, j) if e == 0 else source(1, e, j)).wait_send()

        return carry

    lax.fori_loop(0, CHUNKS, drain, 0)
    for r in range(rounds):
        exchange(r).wait_send()


def solution(mesh):
    n = mesh.shape["gz"]
    rounds = n.bit_length() - 1

    def on_device(coefficient, initial_field, observed, misfit_weight):
        planes, ny, nx = coefficient.shape
        slab = jax.ShapeDtypeStruct(coefficient.shape, jnp.float32)
        exchanges = 2 * ITERS
        grad, adj, misfit = pl.pallas_call(
            functools.partial(kernel, n, rounds, float(n * planes * ny * nx)),
            out_shape=(slab, slab, jax.ShapeDtypeStruct((8, 128), jnp.float32)),
            in_specs=[pl.BlockSpec(memory_space=pl.ANY)] * 4,
            out_specs=[pl.BlockSpec(memory_space=pltpu.VMEM)] * 3,
            scratch_shapes=[
                pltpu.VMEM((exchanges, planes, ny + 2 * PAD, nx), jnp.float32),
                pltpu.VMEM((ITERS - 1, planes, ny, nx), jnp.float32),
                pltpu.VMEM((2, exchanges, ny, nx), jnp.float32),
                pltpu.VMEM((planes, ny, nx), jnp.float32),
                pltpu.VMEM((planes, ny, nx), jnp.float32),
                pltpu.VMEM((planes, ny, nx), jnp.float32),
                pltpu.VMEM((2 * max(rounds, 1), 8, 128), jnp.float32),
                pltpu.SemaphoreType.DMA((2, exchanges, CHUNKS)),
                pltpu.SemaphoreType.DMA((2, exchanges, CHUNKS)),
                pltpu.SemaphoreType.DMA((max(rounds, 1),)),
                pltpu.SemaphoreType.DMA((max(rounds, 1),)),
                pltpu.SemaphoreType.DMA((4,)),
            ],
            compiler_params=pltpu.CompilerParams(
                collective_id=0, has_side_effects=True, vmem_limit_bytes=67043328
            ),
        )(coefficient, initial_field, observed, misfit_weight)
        scale = misfit[0, 0]
        return grad / scale, adj / scale, scale

    placed = P("gz", None, None)
    return jax.shard_map(
        on_device,
        mesh=mesh,
        in_specs=(placed,) * 4,
        out_specs=(placed, placed, P()),
        check_vma=False,
    )
```

time: 297 us -> 209 us (0.70)
  the two profiles are of different devices: /device:TPU:0 before, /device:TPU:14 now
where the time goes in v1:
time: 209 us
  Pallas kernels  202 us (97%)
  other arithmetic  5.38 us (3%)
    pallas_call x1, Pallas kernels, on_device(): pl.pallas_call(functools.partial(kernel, n, rounds, float(n * planes * ny...  202 us
    div x1, other arithmetic, on_device(): return (grad / scale, adj / scale, scale)  5.38 us

profile of v1, /device:TPU:14, one launch (start us, length us, event | category | flops | bytes accessed | tf_op | source)
XLA Modules:
  0.0 209.3 jit_solution(4657556696652279298)
XLA Ops:
  0.6 202.1 %shard_map.67 = (f32[2,512,512]{2,1,0:T(8,128)}, f32[2,512,512]{2,1,0:T(8,128)}, f32[8,128]{1,0:T(8,128)}) custom-call(f32[2,512,512]{2,1,0:T(8,128)} %coef_hbm.1, f32[2,512,512]{2,1,0:T(8,128)} %init_hbm.1, f32[2,512,512]{2,1,0:T(8,128)} %obs_hbm.1, f32[2,512,512]{2,1,0:T(8,128)} %wgt_hbm.1), custom_call_target="tpu_custom_call" | custom-call | tf_op jit(solution)/shard_map/pallas_call | solution.py:317
  202.7 1.2 slice.3
  203.9 5.4 %broadcast_divide_fusion = (f32[2,512,512]{2,1,0:T(8,128)}, f32[2,512,512]{2,1,0:T(8,128)}) fusion(f32[2,512,512]{2,1,0:T(8,128)} %get-tuple-element.8, f32[]{:T(128)} %bitcast, f32[2,512,512]{2,1,0:T(8,128)} %get-tuple-element.6), kind=kLoop, calls=%fused_computation | loop fusion | flops 1048576 | bytes 8388612 | tf_op jit(solution)/shard_map/div | solution.py:341

commit v2 on v0

v2 whole, which is shorter than its diff:
```python
import functools

import jax
import jax.numpy as jnp
from jax import lax
from jax.experimental import pallas as pl
from jax.experimental.pallas import tpu as pltpu
from jax.sharding import PartitionSpec as P

ITERS = 4
time_step = 0.125
MESH = pl.DeviceIdType.MESH
PAD = 8
TILE = 8
CHUNKS = 16


def kernel(n, rounds, cells, coef_hbm, init_hbm, obs_hbm, wgt_hbm, grad_out, adj_out, misfit_out,
           st, sl, halo, coef, obs, wgt, gacc, aacc, acc, part, edge_out, edge_in,
           in_send, in_recv, halo_send, halo_recv, edge_send, edge_recv,
           out_send, out_recv, psend_sem, precv_sem):
    own, ny, nx = coef_hbm.shape
    planes, half = 2 * own, ny // 2
    rows = half // CHUNKS
    exchanges = 2 * ITERS
    me = lax.axis_index("gz")
    q = me % 4
    base = me - q
    h, s = q // 2, q % 2
    lower, upper = me - 3 + 2 * s, me + 1 + 2 * s
    mate = me + 2 - 4 * h
    has_lo = lower >= 0
    has_hi = upper < n
    partners = []
    for r in range(rounds):
        bit = 1 << r
        partners.append(me + bit * (1 - 2 * ((me // bit) % 2)))

    barrier = pltpu.get_barrier_semaphore()

    def greet(device):
        pl.semaphore_signal(barrier, inc=1, device_id=(device,), device_id_type=MESH)

    for i in range(1, 4):
        greet(base + (q + i) % 4)
    for partner in partners[2:]:
        greet(partner)
    outside_lo = (s == 0) & has_lo
    outside_hi = (s == 1) & has_hi

    @pl.when(outside_lo)
    def _():
        greet(lower)

    @pl.when(outside_hi)
    def _():
        greet(upper)

    zero_rows = jnp.zeros((PAD, nx), jnp.float32)
    outer = pl.multiple_of(h * (PAD + half), PAD)
    inner = pl.multiple_of((1 - h) * (PAD + half), PAD)

    def clear_pad(e, carry):
        for p in range(planes):
            st[e, p, pl.ds(outer, PAD), :] = zero_rows
        return carry

    lax.fori_loop(0, exchanges, clear_pad, 0)

    def clear_halo(side):
        def clear(i, carry):
            e = i // (half // PAD)
            row = pl.multiple_of((i % (half // PAD)) * PAD, PAD)
            halo[side, e, pl.ds(row, PAD), :] = zero_rows
            return carry

        lax.fori_loop(0, exchanges * (half // PAD), clear, 0)

    @pl.when(jnp.logical_not(has_lo))
    def _():
        clear_halo(0)

    @pl.when(jnp.logical_not(has_hi))
    def _():
        clear_halo(1)

    acc[...] = jnp.zeros_like(acc)
    crossing = outside_lo | outside_hi

    @pl.when(crossing)
    def _():
        pl.semaphore_wait(barrier, rounds + 2)

    @pl.when(jnp.logical_not(crossing))
    def _():
        pl.semaphore_wait(barrier, rounds + 1)

    hbm = (init_hbm, coef_hbm, obs_hbm, wgt_hbm)
    held = (None, coef, obs, wgt)

    def place(side_half, j):
        return j if side_half == 1 else CHUNKS - 1 - j

    def feed(array, j):
        for to in range(2):
            dest = base + 2 * to + q // 2
            row = place(to, j) * rows
            slot = pl.ds(s * own, own)
            if array == 0:
                if isinstance(j, int) and j == 0:
                    start = row if to == 0 else half - PAD
                    src = init_hbm.at[:, pl.ds(start, rows + PAD), :]
                    dst = st.at[0, slot, pl.ds(PAD + row if to == 0 else 0, rows + PAD), :]
                else:
                    src = init_hbm.at[:, pl.ds(pl.multiple_of(to * half + row, PAD), rows), :]
                    dst = st.at[0, slot, pl.ds(pl.multiple_of(PAD + row, PAD), rows), :]
            else:
                src = hbm[array].at[:, pl.ds(pl.multiple_of(to * half + row, PAD), rows), :]
                dst = held[array].at[slot, pl.ds(pl.multiple_of(row, PAD), rows), :]
            arrived = in_recv.at[array, s, j]

            @pl.when(dest == me)
            def _():
                pltpu.make_async_copy(src, dst, arrived).start()

            @pl.when(dest != me)
            def _():
                pltpu.make_async_remote_copy(
                    src_ref=src, dst_ref=dst, send_sem=in_send.at[array, to], recv_sem=arrived,
                    device_id=(dest,), device_id_type=MESH,
                ).start()

    def await_copy(ref, sem):
        pltpu.make_async_copy(ref, ref, sem).wait()

    def fed(array, j, at):
        for slot in range(2):
            arrived = in_recv.at[array, slot, j]
            mine = pl.ds(slot * own, own)
            if array == 0:
                @pl.when(j == 0)
                def _():
                    start = pl.multiple_of((1 - h) * (PAD + at), PAD)
                    await_copy(st.at[0, mine, pl.ds(start, rows + PAD), :], arrived)

                @pl.when(j != 0)
                def _():
                    await_copy(st.at[0, mine, pl.ds(pl.multiple_of(PAD + at, PAD), rows), :], arrived)
            else:
                await_copy(held[array].at[mine, pl.ds(at, rows), :], arrived)

    for j in range(2):
        feed(0, j)
        feed(1, j)

    def send(e, at, j):
        here = pl.ds(at, rows)
        padded = pl.ds(pl.multiple_of(PAD + at, PAD), rows)

        def copy(side, device):
            pltpu.make_async_remote_copy(
                src_ref=st.at[e, (planes - 1) * (1 - side), padded, :],
                dst_ref=halo.at[side, e, here, :],
                send_sem=halo_send.at[side, e], recv_sem=halo_recv.at[side, e, j],
                device_id=(device,), device_id_type=MESH,
            ).start()

        @pl.when(has_hi)
        def _():
            copy(0, upper)

        @pl.when(has_lo)
        def _():
            copy(1, lower)

    def receive(e, at, j):
        here = pl.ds(at, rows)

        @pl.when(has_lo)
        def _():
            await_copy(halo.at[0, e, here, :], halo_recv.at[0, e, j])

        @pl.when(has_hi)
        def _():
            await_copy(halo.at[1, e, here, :], halo_recv.at[1, e, j])

    def edge_copy(e):
        return pltpu.make_async_remote_copy(
            src_ref=edge_out.at[e], dst_ref=edge_in.at[e],
            send_sem=edge_send.at[e], recv_sem=edge_recv.at[e],
            device_id=(mate,), device_id_type=MESH,
        )

    def stage_edge(e):
        at = pl.multiple_of(PAD + (1 - h) * (half - PAD), PAD)
        for p in range(planes):
            block = st[e, p, pl.ds(at, PAD), :]
            edge_out[e, p:p + 1, :] = jnp.where(h == 0, block[PAD - 1:PAD], block[0:1])

    def take_edge(e):
        edge_copy(e).wait_recv()
        for p in range(planes):
            st[e, p, pl.ds(inner, PAD), :] = jnp.broadcast_to(edge_in[e, p:p + 1, :], (PAD, nx))

    lane = lax.broadcasted_iota(jnp.int32, (TILE, nx), 1)
    leftmost = lane == 0
    rightmost = lane == nx - 1

    def laplace(e, p, row):
        here = pl.ds(row, TILE)
        padded = pl.ds(pl.multiple_of(row + PAD, PAD), TILE)
        tall = st[e, p, pl.ds(row, TILE + 2 * PAD), :]
        mid = tall[PAD:PAD + TILE]
        beside = tall[PAD + 1:PAD + 1 + TILE] + tall[PAD - 1:PAD - 1 + TILE]
        beside = beside + jnp.where(rightmost, 0.0, pltpu.roll(mid, nx - 1, 1))
        beside = beside + jnp.where(leftmost, 0.0, pltpu.roll(mid, 1, 1))
        above = st[e, p + 1, padded, :] if p + 1 < planes else halo[1, e, here, :]
        below = st[e, p - 1, padded, :] if p > 0 else halo[0, e, here, :]
        return mid, beside + above + below - 6.0 * mid

    def ship(which, source, target, at):
        for o in range(2):
            dest = base + 2 * s + o
            src = source.at[pl.ds(o * own, own), pl.ds(at, rows), :]
            dst = target.at[:, pl.ds(pl.multiple_of(h * half + at, PAD), rows), :]

            @pl.when(dest == me)
            def _():
                pltpu.make_async_copy(src, dst, out_recv.at[which, h]).start()

            @pl.when(dest != me)
            def _():
                pltpu.make_async_remote_copy(
                    src_ref=src, dst_ref=dst, send_sem=out_send.at[which, o],
                    recv_sem=out_recv.at[which, h], device_id=(dest,), device_id_type=MESH,
                ).start()

    def stage(e, j):
        at = pl.multiple_of((CHUNKS - 1 - j) * (1 - h) * rows + j * h * rows, PAD)
        if e == 0:
            fed(1, j, at)
        else:
            @pl.when(j == 0)
            def _():
                take_edge(e)
        if e == ITERS - 1:
            fed(2, j, at)
            fed(3, j, at)
        receive(e, at, j)

        def tile(t, carry):
            row = pl.multiple_of(at + t * TILE, TILE)
            here = pl.ds(row, TILE)
            padded = pl.ds(pl.multiple_of(row + PAD, PAD), TILE)
            for p in range(planes):
                mid, slope = laplace(e, p, row)
                if e < ITERS - 1:
                    sl[e, p, here, :] = slope
                    st[e + 1, p, padded, :] = mid + time_step * coef[p, here, :] * slope
                elif e == ITERS - 1:
                    c = coef[p, here, :]
                    resid = mid + time_step * c * slope - obs[p, here, :]
                    weighted = wgt[p, here, :] * resid
                    acc[...] += weighted * resid
                    aacc[p, here, :] = weighted
                    gacc[p, here, :] = time_step * weighted * slope
                    st[e + 1, p, padded, :] = c * weighted
                else:
                    lam = aacc[p, here, :] + time_step * slope
                    aacc[p, here, :] = lam
                    if e < exchanges - 1:
                        gacc[p, here, :] += time_step * lam * sl[exchanges - 2 - e, p, here, :]
                        st[e + 1, p, padded, :] = coef[p, here, :] * lam
            return carry

        lax.fori_loop(0, rows // TILE, tile, 0)
        if e < exchanges - 1:
            @pl.when(j == 0)
            def _():
                stage_edge(e + 1)

            send(e + 1, at, j)

            @pl.when(j == 0)
            def _():
                edge_copy(e + 1).start()
        if e == exchanges - 2:
            ship(0, gacc, grad_out, at)
        if e == exchanges - 1:
            ship(1, aacc, adj_out, at)

    def exchange(r):
        return pltpu.make_async_remote_copy(
            src_ref=part.at[2 * r], dst_ref=part.at[2 * r + 1],
            send_sem=psend_sem.at[r], recv_sem=precv_sem.at[r],
            device_id=(partners[r],), device_id_type=MESH,
        )

    def total_round(r):
        if r == 0:
            whole = acc[...]
            narrow = whole[:, 0:128]
            for i in range(1, nx // 128):
                narrow = narrow + whole[:, 128 * i:128 * i + 128]
            part[0] = narrow
        else:
            exchange(r - 1).wait_recv()
            part[2 * r] = part[2 * r - 2] + part[2 * r - 1]
        exchange(r).start()

    summed = CHUNKS + ITERS - 1
    ticks = CHUNKS + exchanges

    def tick(t, carry):
        @pl.when(t < CHUNKS)
        def _():
            at = pl.multiple_of((CHUNKS - 1 - t) * (1 - h) * rows + t * h * rows, PAD)
            fed(0, t, at)
            send(0, at, t)

        for e in range(exchanges):
            j = t - 1 - e

            @pl.when((j >= 0) & (j < CHUNKS))
            def _():
                stage(e, j)

        @pl.when(t + 2 < CHUNKS)
        def _():
            feed(0, t + 2)
            feed(1, t + 2)

        late = t + 1 - ITERS + 1

        @pl.when((late >= 0) & (late < CHUNKS))
        def _():
            feed(2, late)
            feed(3, late)

        for r in range(min(rounds, ticks - summed)):
            @pl.when(t == summed + r)
            def _():
                total_round(r)

        return carry

    lax.fori_loop(0, ticks, tick, 0)
    for r in range(ticks - summed, rounds):
        total_round(r)

    exchange(rounds - 1).wait_recv()
    whole = part[2 * rounds - 2] + part[2 * rounds - 1]
    whole = jnp.sum(jnp.sum(whole, axis=1, keepdims=True), axis=0, keepdims=True)
    misfit_out[...] = jnp.sqrt(jnp.broadcast_to(whole, (8, 128)) / cells + 1e-06)

    for which, target in enumerate((grad_out, adj_out)):
        for side in range(2):
            await_copy(target.at[:, pl.ds(side * half, half), :], out_recv.at[which, side])
    for which, source in enumerate((gacc, aacc)):
        for o in range(2):
            @pl.when(base + 2 * s + o != me)
            def _():
                await_copy(source.at[pl.ds(o * own, own)], out_send.at[which, o])
    for array in range(4):
        for to in range(2):
            @pl.when(base + 2 * to + q // 2 != me)
            def _():
                extra = PAD if array == 0 else 0
                await_copy(hbm[array].at[:, pl.ds(0, half + extra), :], in_send.at[array, to])
    for e in range(exchanges):
        @pl.when(has_hi)
        def _():
            await_copy(halo.at[0, e], halo_send.at[0, e])

        @pl.when(has_lo)
        def _():
            await_copy(halo.at[1, e], halo_send.at[1, e])
    for e in range(1, exchanges):
        edge_copy(e).wait_send()
    for r in range(rounds):
        exchange(r).wait_send()


def solution(mesh):
    n = mesh.shape["gz"]
    rounds = n.bit_length() - 1

    def on_device(coefficient, initial_field, observed, misfit_weight):
        own, ny, nx = coefficient.shape
        planes, half = 2 * own, ny // 2
        slab = jax.ShapeDtypeStruct(coefficient.shape, jnp.float32)
        exchanges = 2 * ITERS
        block = pltpu.VMEM((planes, half, nx), jnp.float32)
        edge = pltpu.VMEM((exchanges, -(-planes // 8) * 8, nx), jnp.float32)
        dma = pltpu.SemaphoreType.DMA
        grad, adj, misfit = pl.pallas_call(
            functools.partial(kernel, n, rounds, float(n * own * ny * nx)),
            out_shape=(slab, slab, jax.ShapeDtypeStruct((8, 128), jnp.float32)),
            in_specs=[pl.BlockSpec(memory_space=pl.ANY)] * 4,
            out_specs=[pl.BlockSpec(memory_space=pltpu.VMEM)] * 3,
            scratch_shapes=[
                pltpu.VMEM((exchanges, planes, half + 2 * PAD, nx), jnp.float32),
                pltpu.VMEM((ITERS - 1, planes, half, nx), jnp.float32),
                pltpu.VMEM((2, exchanges, half, nx), jnp.float32),
                block, block, block, block, block,
                pltpu.VMEM((TILE, nx), jnp.float32),
                pltpu.VMEM((2 * rounds, 8, 128), jnp.float32),
                edge, edge,
                dma((4, 2)), dma((4, 2, CHUNKS)),
                dma((2, exchanges)), dma((2, exchanges, CHUNKS)),
                dma((exchanges,)), dma((exchanges,)),
                dma((2, 2)), dma((2, 2)),
                dma((rounds,)), dma((rounds,)),
            ],
            compiler_params=pltpu.CompilerParams(
                collective_id=0, has_side_effects=True, vmem_limit_bytes=67043328
            ),
        )(coefficient, initial_field, observed, misfit_weight)
        scale = misfit[0, 0]
        return grad / scale, adj / scale, scale

    placed = P("gz", None, None)
    return jax.shard_map(
        on_device,
        mesh=mesh,
        in_specs=(placed,) * 4,
        out_specs=(placed, placed, P()),
        check_vma=False,
    )
```

time: 297 us -> 163 us (0.55)
  starting transfers between devices: 177 us -> 0 us
  Pallas kernels: 0 us -> 156 us
  blocking collectives: 54.6 us -> 0 us
  other arithmetic: 36.1 us -> 5.38 us
  waiting for transfers between devices: 20.3 us -> 0 us
  local copies, waits for them, and re-layouts: 5.49 us -> 1.19 us
    ppermute x16 -> x0, starting transfers between devices: 177 us -> none  [the longest x8 100 us: shifted(): return lax.ppermute(block, axis, route)]
    pallas_call x0 -> x1, Pallas kernels: none -> 156 us  [on_device(): pl.pallas_call(functools.partial(kernel, n, rounds, float(n * own * ny *...]
    psum x1 -> x0, blocking collectives: 54.6 us -> none  [on_device(): total = lax.psum(jnp.sum(weighted * resid), 'gz')]
    ppermute x16 -> x0, waiting for transfers between devices: 20.3 us -> none  [the longest x8 11.5 us: shifted(): return lax.ppermute(block, axis, route)]
    add x3 -> x0, other arithmetic: 9.57 us -> none  [on_device(): state = state + time_step * coefficient * slope]
    mul x4 -> x0, other arithmetic: 8.65 us -> none  [on_device(): adjoint = adjoint + time_step * adjoint_slope(coefficient * adjoint)]
    div x1, other arithmetic: 13.1 us -> 5.38 us  [on_device(): return (grad / scale, adj / scale, scale)]
    sub x1 -> x0, other arithmetic: 3.56 us -> none  [on_device(): resid = state - observed]
  transfers between devices with their start and end apart: 16 -> 0, of which waited for: 13 -> 0; matrix products, arithmetic and copies ran while one was open for 0% -> 0% of each run, Pallas kernels for 0% -> 0%
where the time goes in v2:
time: 163 us
  Pallas kernels  156 us (96%)
  other arithmetic  5.38 us (3%)
    pallas_call x1, Pallas kernels, on_device(): pl.pallas_call(functools.partial(kernel, n, rounds, float(n * own * ny *...  156 us
    div x1, other arithmetic, on_device(): return (grad / scale, adj / scale, scale)  5.38 us

profile of v2, /device:TPU:0, one launch (start us, length us, event | category | flops | bytes accessed | tf_op | source)
XLA Modules:
  0.0 163.3 jit_solution(15541340213612070546)
XLA Ops:
  0.6 156.1 %shard_map.67 = (f32[2,512,512]{2,1,0:T(8,128)}, f32[2,512,512]{2,1,0:T(8,128)}, f32[8,128]{1,0:T(8,128)}) custom-call(f32[2,512,512]{2,1,0:T(8,128)} %coef_hbm.1, f32[2,512,512]{2,1,0:T(8,128)} %init_hbm.1, f32[2,512,512]{2,1,0:T(8,128)} %obs_hbm.1, f32[2,512,512]{2,1,0:T(8,128)} %wgt_hbm.1), custom_call_target="tpu_custom_call" | custom-call | tf_op jit(solution)/shard_map/pallas_call | solution.py:396
  156.7 1.2 slice.3
  157.9 5.4 %broadcast_divide_fusion = (f32[2,512,512]{2,1,0:T(8,128)}, f32[2,512,512]{2,1,0:T(8,128)}) fusion(f32[2,512,512]{2,1,0:T(8,128)} %get-tuple-element.8, f32[]{:T(128)} %bitcast, f32[2,512,512]{2,1,0:T(8,128)} %get-tuple-element.6), kind=kLoop, calls=%fused_computation | loop fusion | flops 1048576 | bytes 8388612 | tf_op jit(solution)/shard_map/div | solution.py:420

commit v3 on v2

--- a/solution.py
+++ b/solution.py
@@ -60,31 +60,6 @@
     outer = pl.multiple_of(h * (PAD + half), PAD)
     inner = pl.multiple_of((1 - h) * (PAD + half), PAD)
 
-    def clear_pad(e, carry):
-        for p in range(planes):
-            st[e, p, pl.ds(outer, PAD), :] = zero_rows
-        return carry
-
-    lax.fori_loop(0, exchanges, clear_pad, 0)
-
-    def clear_halo(side):
-        def clear(i, carry):
-            e = i // (half // PAD)
-            row = pl.multiple_of((i % (half // PAD)) * PAD, PAD)
-            halo[side, e, pl.ds(row, PAD), :] = zero_rows
-            return carry
-
-        lax.fori_loop(0, exchanges * (half // PAD), clear, 0)
-
-    @pl.when(jnp.logical_not(has_lo))
-    def _():
-        clear_halo(0)
-
-    @pl.when(jnp.logical_not(has_hi))
-    def _():
-        clear_halo(1)
-
-    acc[...] = jnp.zeros_like(acc)
     crossing = outside_lo | outside_hi
 
     @pl.when(crossing)
@@ -149,10 +124,35 @@
             else:
                 await_copy(held[array].at[mine, pl.ds(at, rows), :], arrived)
 
-    for j in range(2):
+    for j in range(3):
         feed(0, j)
         feed(1, j)
 
+    def clear_pad(e, carry):
+        for p in range(planes):
+            st[e, p, pl.ds(outer, PAD), :] = zero_rows
+        return carry
+
+    lax.fori_loop(0, exchanges, clear_pad, 0)
+
+    def clear_halo(side):
+        def clear(i, carry):
+            e = i // (half // PAD)
+            row = pl.multiple_of((i % (half // PAD)) * PAD, PAD)
+            halo[side, e, pl.ds(row, PAD), :] = zero_rows
+            return carry
+
+        lax.fori_loop(0, exchanges * (half // PAD), clear, 0)
+
+    @pl.when(jnp.logical_not(has_lo))
+    def _():
+        clear_halo(0)
+
+    @pl.when(jnp.logical_not(has_hi))
+    def _():
+        clear_halo(1)
+
+    acc[...] = jnp.zeros_like(acc)
     def send(e, at, j):
         here = pl.ds(at, rows)
         padded = pl.ds(pl.multiple_of(PAD + at, PAD), rows)
@@ -218,11 +218,12 @@
         below = st[e, p - 1, padded, :] if p > 0 else halo[0, e, here, :]
         return mid, beside + above + below - 6.0 * mid
 
-    def ship(which, source, target, at):
+    def ship(which, source, target, m):
+        at = pl.multiple_of((CHUNKS - 2 - 2 * m) * (1 - h) * rows + 2 * m * h * rows, PAD)
         for o in range(2):
             dest = base + 2 * s + o
-            src = source.at[pl.ds(o * own, own), pl.ds(at, rows), :]
-            dst = target.at[:, pl.ds(pl.multiple_of(h * half + at, PAD), rows), :]
+            src = source.at[pl.ds(o * own, own), pl.ds(at, 2 * rows), :]
+            dst = target.at[:, pl.ds(pl.multiple_of(h * half + at, PAD), 2 * rows), :]
 
             @pl.when(dest == me)
             def _():
@@ -284,10 +285,6 @@
             @pl.when(j == 0)
             def _():
                 edge_copy(e + 1).start()
-        if e == exchanges - 2:
-            ship(0, gacc, grad_out, at)
-        if e == exchanges - 1:
-            ship(1, aacc, adj_out, at)
 
     def exchange(r):
         return pltpu.make_async_remote_copy(
@@ -325,17 +322,24 @@
             def _():
                 stage(e, j)
 
-        @pl.when(t + 2 < CHUNKS)
-        def _():
-            feed(0, t + 2)
-            feed(1, t + 2)
-
-        late = t + 1 - ITERS + 1
+        @pl.when(t + 3 < CHUNKS)
+        def _():
+            feed(0, t + 3)
+            feed(1, t + 3)
+
+        late = t + 2 - ITERS + 1
 
         @pl.when((late >= 0) & (late < CHUNKS))
         def _():
             feed(2, late)
             feed(3, late)
+
+        for which, source, target, begin in ((0, gacc, grad_out, CHUNKS - 1), (1, aacc, adj_out, CHUNKS - 0)):
+            m = t - begin
+
+            @pl.when((m >= 0) & (m < CHUNKS // 2))
+            def _():
+                ship(which, source, target, m)
 
         for r in range(min(rounds, ticks - summed)):
             @pl.when(t == summed + r)
@@ -391,13 +395,13 @@
         slab = jax.ShapeDtypeStruct(coefficient.shape, jnp.float32)
         exchanges = 2 * ITERS
         block = pltpu.VMEM((planes, half, nx), jnp.float32)
-        edge = pltpu.VMEM((exchanges, -(-planes // 8) * 8, nx), jnp.float32)
+        edge = pltpu.VMEM((exchanges, planes, nx), jnp.float32)
         dma = pltpu.SemaphoreType.DMA
         grad, adj, misfit = pl.pallas_call(
             functools.partial(kernel, n, rounds, float(n * own * ny * nx)),
             out_shape=(slab, slab, jax.ShapeDtypeStruct((8, 128), jnp.float32)),
             in_specs=[pl.BlockSpec(memory_space=pl.ANY)] * 4,
-            out_specs=[pl.BlockSpec(memory_space=pltpu.VMEM)] * 3,
+            out_specs=[pl.BlockSpec(memory_space=pl.ANY)] * 2 + [pl.BlockSpec(memory_space=pltpu.VMEM)],
             scratch_shapes=[
                 pltpu.VMEM((exchanges, planes, half + 2 * PAD, nx), jnp.float32),
                 pltpu.VMEM((ITERS - 1, planes, half, nx), jnp.float32),
@@ -413,7 +417,7 @@
                 dma((rounds,)), dma((rounds,)),
             ],
             compiler_params=pltpu.CompilerParams(
-                collective_id=0, has_side_effects=True, vmem_limit_bytes=67043328
+                collective_id=0, has_side_effects=True, vmem_limit_bytes=48 * 1024 * 1024
             ),
         )(coefficient, initial_field, observed, misfit_weight)
         scale = misfit[0, 0]

time: 163 us -> 153 us (0.939); the launches traced: 163 us -> 151 us
  Pallas kernels: 156 us -> 147 us
  other arithmetic: 5.38 us -> 3.16 us
    pallas_call x1, Pallas kernels: 156 us -> 147 us  [on_device(): pl.pallas_call(functools.partial(kernel, n, rounds, float(n * own * ny *...]
    div x1, other arithmetic: 5.38 us -> 3.16 us  [on_device(): return (grad / scale, adj / scale, scale)]
where the time goes in v3:
time: 153 us; the launch traced here: 151 us
  Pallas kernels  147 us (96%)
  other arithmetic  3.16 us (2%)
    pallas_call x1, Pallas kernels, on_device(): pl.pallas_call(functools.partial(kernel, n, rounds, float(n * own * ny *...  147 us
    div x1, other arithmetic, on_device(): return (grad / scale, adj / scale, scale)  3.16 us

profile of v3, /device:TPU:0, one launch (start us, length us, event | category | flops | bytes accessed | tf_op | source)
XLA Modules:
  0.0 151.3 jit_solution(7170410435442263813)
XLA Ops:
  0.6 147.0 %shard_map.67 = (f32[2,512,512]{2,1,0:T(8,128)S(1)}, f32[2,512,512]{2,1,0:T(8,128)S(1)}, f32[8,128]{1,0:T(8,128)S(1)}) custom-call(f32[2,512,512]{2,1,0:T(8,128)} %coef_hbm.1, f32[2,512,512]{2,1,0:T(8,128)} %init_hbm.1, f32[2,512,512]{2,1,0:T(8,128)} %obs_hbm.1, f32[2,512,512]{2,1,0:T(8,128)} %wgt_hbm.1), custom_call_target="tpu_custom_call" | custom-call | tf_op jit(solution)/shard_map/pallas_call | solution.py:400
  147.6 0.5 slice.3
  148.2 3.2 %broadcast_divide_fusion = (f32[2,512,512]{2,1,0:T(8,128)}, f32[2,512,512]{2,1,0:T(8,128)}) fusion(f32[2,512,512]{2,1,0:T(8,128)S(1)} %get-tuple-element.8, f32[]{:T(128)} %bitcast, f32[2,512,512]{2,1,0:T(8,128)S(1)} %get-tuple-element.6), kind=kLoop, calls=%fused_computation | loop fusion | flops 1048576 | bytes 8388612 | tf_op jit(solution)/shard_map/div | solution.py:424

commit v4 on v3

--- a/solution.py
+++ b/solution.py
@@ -334,12 +334,16 @@
             feed(2, late)
             feed(3, late)
 
-        for which, source, target, begin in ((0, gacc, grad_out, CHUNKS - 1), (1, aacc, adj_out, CHUNKS - 0)):
-            m = t - begin
-
-            @pl.when((m >= 0) & (m < CHUNKS // 2))
+        for which, source, target, begin in ((0, gacc, grad_out, CHUNKS - 2), (1, aacc, adj_out, CHUNKS - 1)):
+            m, final = t - begin, CHUNKS // 2 - 1
+
+            @pl.when((m >= 0) & (m < final))
             def _():
                 ship(which, source, target, m)
+
+            @pl.when(m == final + 1)
+            def _():
+                ship(which, source, target, final)
 
         for r in range(min(rounds, ticks - summed)):
             @pl.when(t == summed + r)

time: 153 us -> 152 us (level); the launches traced: 151 us -> 152 us
  no operation moved by 1% of the time
where the time goes in v4:
time: 152 us
  Pallas kernels  148 us (97%)
  other arithmetic  3.16 us (2%)
    pallas_call x1, Pallas kernels, on_device(): pl.pallas_call(functools.partial(kernel, n, rounds, float(n * own * ny *...  148 us
    div x1, other arithmetic, on_device(): return (grad / scale, adj / scale, scale)  3.16 us

profile of v4, /device:TPU:0, one launch (start us, length us, event | category | flops | bytes accessed | tf_op | source)
XLA Modules:
  0.0 152.0 jit_solution(10801964308971221192)
XLA Ops:
  0.6 147.7 %shard_map.67 = (f32[2,512,512]{2,1,0:T(8,128)S(1)}, f32[2,512,512]{2,1,0:T(8,128)S(1)}, f32[8,128]{1,0:T(8,128)S(1)}) custom-call(f32[2,512,512]{2,1,0:T(8,128)} %coef_hbm.1, f32[2,512,512]{2,1,0:T(8,128)} %init_hbm.1, f32[2,512,512]{2,1,0:T(8,128)} %obs_hbm.1, f32[2,512,512]{2,1,0:T(8,128)} %wgt_hbm.1), custom_call_target="tpu_custom_call" | custom-call | tf_op jit(solution)/shard_map/pallas_call | solution.py:404
  148.3 0.5 slice.3
  148.8 3.2 %broadcast_divide_fusion = (f32[2,512,512]{2,1,0:T(8,128)}, f32[2,512,512]{2,1,0:T(8,128)}) fusion(f32[2,512,512]{2,1,0:T(8,128)S(1)} %get-tuple-element.8, f32[]{:T(128)} %bitcast, f32[2,512,512]{2,1,0:T(8,128)S(1)} %get-tuple-element.6), kind=kLoop, calls=%fused_computation | loop fusion | flops 1048576 | bytes 8388612 | tf_op jit(solution)/shard_map/div | solution.py:428
